TPU v7x, 32 devices: a whole 2x2x4 slice. The times are simulated.
32 devices in a mesh: energy: 8 (over z, y), slab: 4 (over x, core).
Axes of the slice: x: 2, y: 2, z: 4, core: 2. Of those that a mesh axis runs over, the one named last changes fastest.
Arguments:
- green_blocks: bfloat16 [16, 4, 512, 512], P('energy', 'slab'), may hold values from -6 to 6
- coupling: bfloat16 [4, 512, 512], P('slab'), may hold values from -0.25 to 0.25
- coulomb: bfloat16 [4, 512, 512], P('slab'), may hold values from -0.25 to 0.25
Outputs:
- self_energy: bfloat16 [16, 4, 512, 512], P('energy', 'slab')
- screening: bfloat16 [16, 4, 512, 512], P('energy', 'slab')
All inputs are finite; a program needn't handle non-finite values.
Results may differ from a plain program's by a relative error of at most 0.0075.
Values may be sent and summed in bfloat16 or wider, within the bound.
A program may use at most 64 MiB of HBM per device.

v0:
```python
import math

import jax
import jax.numpy as jnp
from jax import lax
from jax.sharding import PartitionSpec as P


def from_behind(block, axis, distance):
    devices = range(lax.axis_size(axis))
    route = [(i - distance, i) for i in devices if i - distance in devices]
    return lax.ppermute(block, axis, route)


def with_halo(array, sides, width):
    for axis, dim in sides:
        count, length = (lax.axis_size(axis), array.shape[dim])
        up = [(i, (i + 1) % count) for i in range(count - 1)]
        down = [(j, i) for i, j in up]
        last = lax.slice_in_dim(array, length - width, length, axis=dim)
        leading = lax.slice_in_dim(array, 0, width, axis=dim)
        before = lax.ppermute(last, axis, up)
        after = lax.ppermute(leading, axis, down)
        array = jnp.concatenate([before, array, after], axis=dim)
    return array


def tables(count):
    indices = jnp.arange(count, dtype=jnp.int32)
    product = indices[:, None] * indices[None, :] % count
    angles = product.astype(jnp.float32) * (2.0 * math.pi / count)
    return (jnp.cos(angles), jnp.sin(angles))


def correlate(blocks):
    count = blocks.shape[0]
    cosine, sine = tables(count)
    flattened = blocks.astype(jnp.float32).reshape(count, -1)
    cosine_part = jnp.dot(cosine, flattened, precision=lax.Precision.HIGHEST)
    sine_part = jnp.dot(sine, flattened, precision=lax.Precision.HIGHEST)
    spectrum = cosine_part * cosine_part + sine_part * sine_part
    folded = jnp.dot(cosine, spectrum, precision=lax.Precision.HIGHEST) * (
        1.0 / (count * math.sqrt(count))
    )
    return folded.reshape(blocks.shape).astype(jnp.bfloat16)


def dress_lower(blocks, link):
    inner = jnp.einsum("eij,jk->eik", blocks, link, preferred_element_type=jnp.float32).astype(
        jnp.bfloat16
    )
    return jnp.einsum("ji,ejk->eik", link, inner, preferred_element_type=jnp.float32).astype(
        jnp.bfloat16
    )


def dress_upper(blocks, link):
    inner = jnp.einsum("eij,kj->eik", blocks, link, preferred_element_type=jnp.float32).astype(
        jnp.bfloat16
    )
    return jnp.einsum("ij,ejk->eik", link, inner, preferred_element_type=jnp.float32).astype(
        jnp.bfloat16
    )


def on_device(green_blocks, coupling, coulomb):
    own_green = green_blocks[:, 0]
    own_link = coupling[0]
    link_below = from_behind(coupling, "slab", 1)[0]
    for_above = dress_lower(own_green, own_link)
    for_below = dress_upper(own_green, link_below)
    lower = from_behind(for_above, "slab", 1)
    upper = from_behind(for_below, "slab", -1)
    sigma = (lower.astype(jnp.float32) + upper.astype(jnp.float32)).astype(jnp.bfloat16)
    entry_rows = lax.all_to_all(green_blocks, "energy", split_axis=2, concat_axis=0, tiled=True)
    polar_rows = correlate(entry_rows)
    polar = lax.all_to_all(polar_rows, "energy", split_axis=0, concat_axis=2, tiled=True)
    polar_rim = with_halo(polar, (("slab", 1),), 1)
    beside = polar_rim[:, 0].astype(jnp.float32) + polar_rim[:, 2].astype(jnp.float32)
    screen_block = coulomb[0]
    inner = jnp.einsum(
        "eij,kj->eik", polar[:, 0], screen_block, preferred_element_type=jnp.float32
    ).astype(jnp.bfloat16)
    outer = jnp.einsum("ij,ejk->eik", screen_block, inner, preferred_element_type=jnp.float32)
    screened = (outer + 0.5 * beside).astype(jnp.bfloat16)
    return (sigma[:, None], screened[:, None])


def solution(mesh):
    placed = (P("energy", "slab", None, None), P("slab", None, None), P("slab", None, None))
    return jax.shard_map(
        on_device,
        mesh=mesh,
        in_specs=placed,
        out_specs=(P("energy", "slab", None, None), P("energy", "slab", None, None)),
        check_vma=False,
    )
```

profile of v0, /device:TPU:1, one launch (start us, length us, event | category | flops | bytes accessed | tf_op | source)
XLA Modules:
  0.0 96.5 jit_solution(1786410056632058825)
XLA Ops:
  0.6 0.0 copy-start
  0.6 2.4 %copy.50 = bf16[2,1,512,512]{3,0,1,2:T(2,128)(2,1)S(1)} copy(bf16[2,1,512,512]{3,2,1,0:T(8,128)(2,1)} %param.3) | data formatting | bytes 2097152 | tf_op args[0]
  3.0 31.0 %all_to_all.33 = bf16[2,1,512,512]{3,0,1,2:T(2,128)(2,1)S(1)} all-to-all(bf16[2,1,512,512]{3,0,1,2:T(2,128)(2,1)S(1)} %copy.50), channel_id=1, replica_groups=mesh['energy'=8,'slab'=4] {'energy'}, dimensions={2} | all-to-all | bytes 2097152 | tf_op jit(solution)/shard_map/all_to_all | solution.py:75
  34.0 0.2 copy.51
  34.2 0.1 copy.52
  34.3 0.6 copy.64
  34.9 1.0 %convolution_multiply_fusion = f32[16,32768]{1,0:T(8,128)S(1)} fusion(bf16[16,32768]{1,0:T(8,128)(2,1)S(1)} %bitcast.62), kind=kOutput, calls=%fused_computation | convolution fusion | flops 101191168 | bytes 3145728 | tf_op jit(solution)/shard_map/dot_general | solution.py:40
  35.9 1.1 %fusion = f32[16,32768]{1,0:T(8,128)S(1)} fusion(f32[16,32768]{1,0:T(8,128)S(1)} %convolution_multiply_fusion, bf16[16,32768]{1,0:T(8,128)(2,1)S(1)} %bitcast.63), kind=kOutput, calls=%fused_computation.2 | convolution fusion | flops 101715456 | bytes 5242880 | tf_op jit(solution)/shard_map/dot_general | solution.py:39
  37.1 1.9 %fusion.1 = bf16[16,32768]{1,0:T(8,128)(2,1)S(1)} fusion(f32[16,32768]{1,0:T(8,128)S(1)} %fusion), kind=kOutput, calls=%fused_computation.4 | convolution fusion | flops 101715456 | bytes 3145728 | tf_op jit(solution)/shard_map/dot_general | solution.py:42
  39.0 0.0 copy-start.2
  39.1 0.0 copy-start.1
  39.1 1.3 %copy.65 = bf16[2,8,64,512]{3,2,1,0:T(8,128)(2,1)} copy(bf16[2,8,64,512]{3,1,2,0:T(8,128)(2,1)S(1)} %bitcast.64) | data formatting | bytes 2097152
  40.4 4.1 %all-to-all-start.1 = ((bf16[16,1,64,512]{3,2,1,0:T(8,128)(2,1)}), bf16[16,1,64,512]{3,2,1,0:T(8,128)(2,1)S(1)}, u32[]{:S(2)}, u32[]{:S(2)}) async-start(bf16[16,1,64,512]{3,2,1,0:T(8,128)(2,1)} %bitcast.10), calls=%async_computation.1 | async-start | bytes 2097152 | tf_op jit(solution)/shard_map/all_to_all | solution.py:77
  44.5 4.3 %collective-permute-start.1 = (bf16[1,512,512]{2,1,0:T(8,128)(2,1)S(1)}, bf16[1,512,512]{2,1,0:T(8,128)(2,1)}, u32[]{:S(2)}, u32[]{:S(2)}) collective-permute-start(bf16[1,512,512]{2,1,0:T(8,128)(2,1)S(1)} %copy-done.2), channel_id=1, source_target_pairs={{0,1},{1,2},{2,3},{4,5},{5,6},{6,7},{8,9},{9,10},{10,11},{12,13},{... | collective-permute-start | bytes 1572872 | tf_op jit(solution)/shard_map/ppermute | solution.py:12
  48.8 2.3 %fusion.4 = bf16[2,512,512]{1,2,0:T(8,128)(2,1)} fusion(bf16[2,1,512,512]{3,2,1,0:T(8,128)(2,1)S(1)} %copy-done.1, bf16[1,512,512]{2,1,0:T(8,128)(2,1)S(1)} %copy-done.2), kind=kOutput, calls=%fused_computation.14 | convolution fusion | flops 1074790400 | bytes 2621440 | tf_op jit(solution)/shard_map/ji,ejk->eik/dot_general | solution.py:52
  51.2 1.9 %collective-permute-start = (bf16[2,512,512]{1,2,0:T(8,128)(2,1)}, bf16[2,512,512]{1,2,0:T(8,128)(2,1)}, u32[]{:S(2)}, u32[]{:S(2)}) collective-permute-start(bf16[2,512,512]{1,2,0:T(8,128)(2,1)} %fusion.4), channel_id=1, source_target_pairs={{0,1},{1,2},{2,3},{4,5},{5,6},{6,7},{8,9},{9,10},{10,11},{12,13},{... | collective-permute-start | bytes 3145736 | tf_op jit(solution)/shard_map/ppermute | solution.py:12
  53.1 1.9 %collective-permute-done.1 = bf16[1,512,512]{2,1,0:T(8,128)(2,1)} collective-permute-done((bf16[1,512,512]{2,1,0:T(8,128)(2,1)S(1)}, bf16[1,512,512]{2,1,0:T(8,128)(2,1)}, u32[]{:S(2)}, u32[]{:S(2)}) %collective-permute-start.1) | collective-permute-done | bytes 524320 | tf_op jit(solution)/shard_map/ppermute | solution.py:12
  54.9 3.5 %fusion.5 = bf16[2,512,512]{1,2,0:T(8,128)(2,1)} fusion(bf16[2,1,512,512]{3,2,1,0:T(8,128)(2,1)S(1)} %copy-done.1, bf16[1,512,512]{2,1,0:T(8,128)(2,1)} %collective-permute-done.1), kind=kOutput, calls=%fused_computation.15 | convolution fusion | flops 1074790400 | bytes 2621440 | tf_op jit(solution)/shard_map/ij,ejk->eik/dot_general | solution.py:61
  58.4 1.9 %collective-permute-start.2 = (bf16[2,512,512]{1,2,0:T(8,128)(2,1)}, bf16[2,512,512]{1,2,0:T(8,128)(2,1)}, u32[]{:S(2)}, u32[]{:S(2)}) collective-permute-start(bf16[2,512,512]{1,2,0:T(8,128)(2,1)} %fusion.5), channel_id=1, source_target_pairs={{1,0},{2,1},{3,2},{5,4},{6,5},{7,6},{9,8},{10,9},{11,10},{13,12},{... | collective-permute-start | bytes 3145736 | tf_op jit(solution)/shard_map/ppermute | solution.py:12
  60.3 8.8 %all-to-all-done.1 = bf16[16,1,64,512]{3,2,1,0:T(8,128)(2,1)S(1)} async-done(((bf16[16,1,64,512]{3,2,1,0:T(8,128)(2,1)}), bf16[16,1,64,512]{3,2,1,0:T(8,128)(2,1)S(1)}, u32[]{:S(2)}, u32[]{:S(2)}) %all-to-all-start.1) | async-done | bytes 1048608 | tf_op jit(solution)/shard_map/all_to_all | solution.py:77
  69.1 0.1 copy.54
  69.2 1.3 %copy.57 = bf16[2,1,512,512]{2,3,0,1:T(8,128)(2,1)} copy(bf16[2,1,512,512]{3,2,0,1:T(8,128)(2,1)S(1)} %bitcast.65) | data formatting | bytes 2097152 | tf_op jit(solution)/shard_map/all_to_all | solution.py:77
  70.5 5.3 %collective-permute-start.3 = (bf16[2,1,512,512]{2,3,0,1:T(8,128)(2,1)}, bf16[2,1,512,512]{2,3,0,1:T(8,128)(2,1)}, u32[]{:S(2)}, u32[]{:S(2)}) collective-permute-start(bf16[2,1,512,512]{2,3,0,1:T(8,128)(2,1)} %copy.57), channel_id=1, source_target_pairs={{0,1},{1,2},{2,3},{4,5},{5,6},{6,7},{8,9},{9,10},{10,11},{12,13},{... | collective-permute-start | bytes 3145736 | tf_op jit(solution)/shard_map/ppermute | solution.py:22
  75.8 1.9 %collective-permute-start.4 = (bf16[2,1,512,512]{2,3,0,1:T(8,128)(2,1)}, bf16[2,1,512,512]{2,3,0,1:T(8,128)(2,1)}, u32[]{:S(2)}, u32[]{:S(2)}) collective-permute-start(bf16[2,1,512,512]{2,3,0,1:T(8,128)(2,1)} %copy.57), channel_id=1, source_target_pairs={{1,0},{2,1},{3,2},{5,4},{6,5},{7,6},{9,8},{10,9},{11,10},{13,12},{... | collective-permute-start | bytes 3145736 | tf_op jit(solution)/shard_map/ppermute | solution.py:23
  77.7 0.0 collective-permute-done
  77.8 0.0 collective-permute-done.2
  77.8 1.8 %fusion.6 = bf16[2,1,512,512]{2,3,0,1:T(8,128)(2,1)S(1)} fusion(bf16[2,512,512]{1,2,0:T(8,128)(2,1)} %collective-permute-done.2, bf16[2,512,512]{1,2,0:T(8,128)(2,1)} %collective-permute-done), kind=kLoop, calls=%fused_computation.16 | loop fusion | flops 2097152 | bytes 3145728 | tf_op jit(solution)/shard_map/broadcast_in_dim | solution.py:86
  79.6 1.3 %copy.59 = bf16[2,1,512,512]{3,2,1,0:T(8,128)(2,1)} copy(bf16[2,1,512,512]{2,3,0,1:T(8,128)(2,1)S(1)} %fusion.6) | data formatting | bytes 2097152
  80.9 6.9 %collective-permute-done.3 = bf16[2,1,512,512]{2,3,0,1:T(8,128)(2,1)} collective-permute-done((bf16[2,1,512,512]{2,3,0,1:T(8,128)(2,1)}, bf16[2,1,512,512]{2,3,0,1:T(8,128)(2,1)}, u32[]{:S(2)}, u32[]{:S(2)}) %collective-permute-start.3) | collective-permute-done | bytes 1048608 | tf_op jit(solution)/shard_map/ppermute | solution.py:22
  87.8 4.4 %collective-permute-done.4 = bf16[2,1,512,512]{2,3,0,1:T(8,128)(2,1)} collective-permute-done((bf16[2,1,512,512]{2,3,0,1:T(8,128)(2,1)}, bf16[2,1,512,512]{2,3,0,1:T(8,128)(2,1)}, u32[]{:S(2)}, u32[]{:S(2)}) %collective-permute-start.4) | collective-permute-done | bytes 1048608 | tf_op jit(solution)/shard_map/ppermute | solution.py:23
  92.2 2.9 %fusion.3 = bf16[2,1,512,512]{2,3,0,1:T(8,128)(2,1)S(1)} fusion(bf16[2,1,512,512]{2,3,0,1:T(8,128)(2,1)} %collective-permute-done.4, bf16[2,1,512,512]{2,3,0,1:T(8,128)(2,1)} %collective-permute-done.3, bf16[2,512,512]{2,1,0:T(8,128)(2,1)S(1)} %bitcast.66, bf16[1,512,512]{2,1,0:T(8,128)(2,1)S(1)} %copy-done), kind=kOutput, calls=%fused_computation.13 | convolution fusion | flops 1077411840 | bytes 4718592 | tf_op jit(solution)/shard_map/ij,ejk->eik/dot_general | solution.py:84
  95.1 1.3 %copy.60 = bf16[2,1,512,512]{3,2,1,0:T(8,128)(2,1)} copy(bf16[2,1,512,512]{2,3,0,1:T(8,128)(2,1)S(1)} %fusion.3) | data formatting | bytes 2097152
  (3 shorter events, 0.0 us)
Async XLA Ops:
  0.6 91.6 %copy-start = (bf16[1,512,512]{2,1,0:T(8,128)(2,1)S(1)}, bf16[1,512,512]{2,1,0:T(8,128)(2,1)}, u32[]{:S(2)}) copy-start(bf16[1,512,512]{2,1,0:T(8,128)(2,1)} %param.5) | copy-start | bytes 1572868
  39.0 5.5 %copy-start.2 = (bf16[1,512,512]{2,1,0:T(8,128)(2,1)S(1)}, bf16[1,512,512]{2,1,0:T(8,128)(2,1)}, u32[]{:S(2)}) copy-start(bf16[1,512,512]{2,1,0:T(8,128)(2,1)} %param.4) | copy-start | bytes 1572868
  39.1 9.8 %copy-start.1 = (bf16[2,1,512,512]{3,2,1,0:T(8,128)(2,1)S(1)}, bf16[2,1,512,512]{3,2,1,0:T(8,128)(2,1)}, u32[]{:S(2)}) copy-start(bf16[2,1,512,512]{3,2,1,0:T(8,128)(2,1)} %param.3) | copy-start | bytes 3145732
  40.4 28.7 %all-to-all-start.1 = ((bf16[16,1,64,512]{3,2,1,0:T(8,128)(2,1)}), bf16[16,1,64,512]{3,2,1,0:T(8,128)(2,1)S(1)}, u32[]{:S(2)}, u32[]{:S(2)}) async-start(bf16[16,1,64,512]{3,2,1,0:T(8,128)(2,1)} %bitcast.10), calls=%async_computation.1 | async-start | bytes 2097152 | tf_op jit(solution)/shard_map/all_to_all | solution.py:77
  44.5 10.4 %collective-permute-start.1 = (bf16[1,512,512]{2,1,0:T(8,128)(2,1)S(1)}, bf16[1,512,512]{2,1,0:T(8,128)(2,1)}, u32[]{:S(2)}, u32[]{:S(2)}) collective-permute-start(bf16[1,512,512]{2,1,0:T(8,128)(2,1)S(1)} %copy-done.2), channel_id=1, source_target_pairs={{0,1},{1,2},{2,3},{4,5},{5,6},{6,7},{8,9},{9,10},{10,11},{12,13},{... | collective-permute-start | bytes 1572872 | tf_op jit(solution)/shard_map/ppermute | solution.py:12
  51.2 26.6 %collective-permute-start = (bf16[2,512,512]{1,2,0:T(8,128)(2,1)}, bf16[2,512,512]{1,2,0:T(8,128)(2,1)}, u32[]{:S(2)}, u32[]{:S(2)}) collective-permute-start(bf16[2,512,512]{1,2,0:T(8,128)(2,1)} %fusion.4), channel_id=1, source_target_pairs={{0,1},{1,2},{2,3},{4,5},{5,6},{6,7},{8,9},{9,10},{10,11},{12,13},{... | collective-permute-start | bytes 3145736 | tf_op jit(solution)/shard_map/ppermute | solution.py:12
  58.4 19.4 %collective-permute-start.2 = (bf16[2,512,512]{1,2,0:T(8,128)(2,1)}, bf16[2,512,512]{1,2,0:T(8,128)(2,1)}, u32[]{:S(2)}, u32[]{:S(2)}) collective-permute-start(bf16[2,512,512]{1,2,0:T(8,128)(2,1)} %fusion.5), channel_id=1, source_target_pairs={{1,0},{2,1},{3,2},{5,4},{6,5},{7,6},{9,8},{10,9},{11,10},{13,12},{... | collective-permute-start | bytes 3145736 | tf_op jit(solution)/shard_map/ppermute | solution.py:12
  70.5 17.3 %collective-permute-start.3 = (bf16[2,1,512,512]{2,3,0,1:T(8,128)(2,1)}, bf16[2,1,512,512]{2,3,0,1:T(8,128)(2,1)}, u32[]{:S(2)}, u32[]{:S(2)}) collective-permute-start(bf16[2,1,512,512]{2,3,0,1:T(8,128)(2,1)} %copy.57), channel_id=1, source_target_pairs={{0,1},{1,2},{2,3},{4,5},{5,6},{6,7},{8,9},{9,10},{10,11},{12,13},{... | collective-permute-start | bytes 3145736 | tf_op jit(solution)/shard_map/ppermute | solution.py:22
  75.8 16.4 %collective-permute-start.4 = (bf16[2,1,512,512]{2,3,0,1:T(8,128)(2,1)}, bf16[2,1,512,512]{2,3,0,1:T(8,128)(2,1)}, u32[]{:S(2)}, u32[]{:S(2)}) collective-permute-start(bf16[2,1,512,512]{2,3,0,1:T(8,128)(2,1)} %copy.57), channel_id=1, source_target_pairs={{1,0},{2,1},{3,2},{5,4},{6,5},{7,6},{9,8},{10,9},{11,10},{13,12},{... | collective-permute-start | bytes 3145736 | tf_op jit(solution)/shard_map/ppermute | solution.py:23
where the time goes:
time: 96.9 us; the launch traced here: 96.5 us
  blocking collectives  31 us (32%)
  waiting for transfers between devices  22 us (23%)
  starting transfers between devices  19.5 us (20%)
  matrix products  12.8 us (13%)
  local copies, waits for them, and re-layouts  8.58 us (9%)
  other arithmetic  1.83 us (2%)
    all_to_all x1, blocking collectives, on_device(): lax.all_to_all(green_blocks, 'energy', split_axis=2, concat_axis=0, tiled...  31 us
    all_to_all x1, waiting for transfers between devices, on_device(): lax.all_to_all(polar_rows, 'energy', split_axis=0, concat_axis=2, tiled=T...  8.81 us
    ppermute x3, starting transfers between devices, from_behind(): return lax.ppermute(block, axis, route)  8.13 us
    ppermute x1, waiting for transfers between devices, with_halo(): before = lax.ppermute(last, axis, up)  6.93 us
    unnamed x11, local copies, waits for them, and re-layouts  6.91 us
    ppermute x1, starting transfers between devices, with_halo(): before = lax.ppermute(last, axis, up)  5.26 us
    ppermute x1, waiting for transfers between devices, with_halo(): after = lax.ppermute(leading, axis, down)  4.4 us
    all_to_all x1, starting transfers between devices, on_device(): lax.all_to_all(polar_rows, 'energy', split_axis=0, concat_axis=2, tiled=T...  4.14 us
  transfers between devices with their start and end apart: 6, of which 4 were waited for; matrix products, arithmetic and copies ran while one was open for 11% of the time, Pallas kernels for 0%

commit v1 on v0

v1 whole, which is shorter than its diff:
```python
import functools

import jax
import jax.numpy as jnp
from jax import lax
from jax.experimental import pallas as pl
from jax.experimental.pallas import tpu as pltpu
from jax.sharding import PartitionSpec as P

MESH = pl.DeviceIdType.MESH
F32, BF16 = jnp.float32, jnp.bfloat16
TILE = 16
LANES = 128


def matmul(a, b, a_dim=1, b_dim=0):
    return lax.dot_general(a, b, (((a_dim,), (b_dim,)), ((), ())), preferred_element_type=F32)


def correlate(gath, prow, row0, rows):
    count, _, m = gath.shape
    scale = float(count) ** -0.5
    across = m // LANES

    def tile(i, _):
        r = pl.ds(pl.multiple_of(row0 + (i // across) * TILE, TILE), TILE)
        l = pl.ds(pl.multiple_of((i % across) * LANES, LANES), LANES)

        def put(w, total):
            value = (total * scale).astype(BF16)
            prow[w, r, l] = value
            return value

        if count <= 16:
            x = [gath[e, r, l].astype(F32) for e in range(count)]
            for w in range(count // 2 + 1):
                if 2 * w == count:
                    terms = [x[e] * x[e + w] for e in range(w)]
                else:
                    terms = [x[e] * x[(e + w) % count] for e in range(count)]
                while len(terms) > 1:
                    terms = [sum(terms[j : j + 2]) for j in range(0, len(terms), 2)]
                total = terms[0] * 2.0 if 2 * w == count else terms[0]
                value = put(w, total)
                if 0 < w < count - w:
                    prow[count - w, r, l] = value
        else:

            def lag(w, _):
                def term(e, total):
                    return total + gath[e, r, l].astype(F32) * gath[(e + w) % count, r, l].astype(F32)

                put(w, lax.fori_loop(0, count, term, jnp.zeros((TILE, LANES), F32)))
                return 0

            lax.fori_loop(0, count, lag, 0)
        return 0

    lax.fori_loop(0, (rows // TILE) * across, tile, 0)


def kernel(
    n, ns, parts, green, coupling, coulomb, sigma_out, screen_out,
    g, h, c, gath, prow, pol, inner, rim_b, rim_a, g_above, low_in, low_out, sigma, screen,
    local, ss1, rs1, ss2, rs2, ssb, rsb, ssa, rsa, sside, rside,
):
    per, m = g.shape[0], g.shape[1]
    rows = m // n // parts
    me, slab = lax.axis_index("energy"), lax.axis_index("slab")
    up, down = jnp.minimum(slab + 1, ns - 1), jnp.maximum(slab - 1, 0)
    has_up, has_down = slab < ns - 1, slab > 0
    order = sorted(range(1, n), key=lambda i: abs(2 * i - n))

    def block(part, owner):
        return pl.ds(pl.multiple_of(part * (m // parts) + owner * rows, rows), rows)

    loads = [
        pltpu.make_async_copy(green.at[:, 0], g, local.at[0]),
        pltpu.make_async_copy(coupling.at[0], h, local.at[1]),
        pltpu.make_async_copy(coulomb.at[0], c, local.at[2]),
    ]
    own = [
        pltpu.make_async_copy(
            green.at[:, 0, block(part, me)],
            gath.at[pl.ds(me * per, per), pl.ds(part * rows, rows)],
            local.at[3 + part],
        )
        for part in range(parts)
    ]
    for copy in loads + own:
        copy.start()

    barrier = pltpu.get_barrier_semaphore()
    for i in range(1, n):
        pl.semaphore_signal(barrier, inc=1, device_id={"energy": (me + i) % n}, device_id_type=MESH)

    @pl.when(has_up)
    def _():
        pl.semaphore_signal(barrier, inc=1, device_id={"slab": up}, device_id_type=MESH)

    @pl.when(has_down)
    def _():
        pl.semaphore_signal(barrier, inc=1, device_id={"slab": down}, device_id_type=MESH)

    pl.semaphore_wait(barrier, n - 1 + has_up.astype(jnp.int32) + has_down.astype(jnp.int32))

    def remote(src, dst, send, recv, where):
        return pltpu.make_async_remote_copy(
            src_ref=src, dst_ref=dst, send_sem=send, recv_sem=recv, device_id=where, device_id_type=MESH
        )

    loads[0].wait()
    first = {}
    for part in range(parts):
        for i in order:
            to = (me + i) % n
            first[part, i] = remote(
                g.at[:, block(part, to)],
                gath.at[pl.ds(me * per, per), pl.ds(part * rows, rows)],
                ss1.at[part, i], rs1.at[part, i], {"energy": to},
            )
            first[part, i].start()

    green_down = remote(g, g_above, sside.at[0], rside.at[0], {"slab": down})
    lower_up = remote(low_out, low_in, sside.at[1], rside.at[1], {"slab": up})

    @pl.when(has_down)
    def _():
        green_down.start()

    @pl.when(jnp.logical_not(has_down))
    def _():
        low_in[...] = jnp.zeros_like(low_in)
        rim_b[...] = jnp.zeros_like(rim_b)

    loads[1].wait()

    def lower(e, _):
        mid = matmul(g[e], h[...]).astype(BF16)
        low_out[e] = matmul(h[...], mid, 0, 0).astype(BF16)
        return 0

    lax.fori_loop(0, per, lower, 0)

    @pl.when(jnp.logical_not(has_up))
    def _():
        g_above[...] = jnp.zeros_like(g_above)
        rim_a[...] = jnp.zeros_like(rim_a)

    @pl.when(has_up)
    def _():
        lower_up.start()

    def self_energy():
        @pl.when(has_up)
        def _():
            green_down.wait_recv()

        @pl.when(has_down)
        def _():
            lower_up.wait_recv()

        def upper(e, _):
            mid = matmul(g_above[e], h[...], 1, 1).astype(BF16)
            term = matmul(h[...], mid).astype(BF16)
            sigma[e] = (low_in[e].astype(F32) + term.astype(F32)).astype(BF16)
            return 0

        lax.fori_loop(0, per, upper, 0)

    second, rims = {}, {}

    def forward(part, i):
        piece = block(part, (me - i + n) % n)
        rims[part, i] = (
            remote(pol.at[:, piece], rim_b.at[:, piece], ssb.at[part, i], rsb.at[part, i], {"slab": up}),
            remote(pol.at[:, piece], rim_a.at[:, piece], ssa.at[part, i], rsa.at[part, i], {"slab": down}),
        )

        @pl.when(has_up)
        def _():
            rims[part, i][0].start()

        @pl.when(has_down)
        def _():
            rims[part, i][1].start()

    for part in range(parts):
        own[part].wait()
        for i in order:
            first[part, i].wait_recv()
        correlate(gath, prow, part * rows, rows)
        span = pl.ds(part * rows, rows)
        pol[:, block(part, me)] = prow[pl.ds(me * per, per), span]
        for i in order:
            to = (me + i) % n
            second[part, i] = remote(
                prow.at[pl.ds(to * per, per), span], pol.at[:, block(part, me)],
                ss2.at[part, i], rs2.at[part, i], {"energy": to},
            )
            second[part, i].start()
        forward(part, 0)
    self_energy()
    sigma_store = pltpu.make_async_copy(sigma, sigma_out.at[:, 0], local.at[0])
    sigma_store.start()

    loads[2].wait()
    for part in range(parts):
        for i in order:
            second[part, i].wait_recv()
            forward(part, i)
        half = pl.ds(part * (m // parts), m // parts)

        def screen_inner(e, _):
            inner[e, half] = matmul(pol[e, half], c[...], 1, 1).astype(BF16)
            return 0

        lax.fori_loop(0, per, screen_inner, 0)

    for copies in rims.values():
        @pl.when(has_down)
        def _():
            copies[0].wait_recv()

        @pl.when(has_up)
        def _():
            copies[1].wait_recv()

    stores = []
    for e in range(per):
        beside = rim_b[e].astype(F32) + rim_a[e].astype(F32)
        screen[e] = (matmul(c[...], inner[e]) + 0.5 * beside).astype(BF16)
        stores.append(pltpu.make_async_copy(screen.at[e], screen_out.at[e, 0], local.at[1 + e]))
        stores[-1].start()

    for copy in list(first.values()) + list(second.values()):
        copy.wait_send()

    @pl.when(has_up)
    def _():
        lower_up.wait_send()
        for copies in rims.values():
            copies[0].wait_send()

    @pl.when(has_down)
    def _():
        green_down.wait_send()
        for copies in rims.values():
            copies[1].wait_send()

    sigma_store.wait()
    for copy in stores:
        copy.wait()


def solution(mesh):
    n, ns = mesh.shape["energy"], mesh.shape["slab"]

    def step(green, coupling, coulomb):
        per, m, count = green.shape[0], green.shape[-1], green.shape[0] * n
        parts = 2 if m // n % (2 * TILE) == 0 else 1
        rows = m // n
        blocks = pltpu.VMEM((per, m, m), BF16)
        square = pltpu.VMEM((m, m), BF16)
        strip = pltpu.VMEM((count, rows, m), BF16)
        sems = pltpu.SemaphoreType.DMA((parts, n))
        anywhere = pl.BlockSpec(memory_space=pl.ANY)
        return tuple(pl.pallas_call(
            functools.partial(kernel, n, ns, parts),
            out_shape=[jax.ShapeDtypeStruct(green.shape, BF16)] * 2,
            in_specs=[anywhere] * 3,
            out_specs=[anywhere] * 2,
            scratch_shapes=[blocks, square, square, strip, strip]
            + [blocks] * 9
            + [pltpu.SemaphoreType.DMA((max(3 + parts, 1 + per),))]
            + [sems] * 8
            + [pltpu.SemaphoreType.DMA((2,))] * 2,
            compiler_params=pltpu.CompilerParams(
                collective_id=0, has_side_effects=True, vmem_limit_bytes=67043328
            ),
        )(green, coupling, coulomb))

    placed = (P("energy", "slab", None, None), P("slab", None, None), P("slab", None, None))
    return jax.shard_map(
        step,
        mesh=mesh,
        in_specs=placed,
        out_specs=(P("energy", "slab", None, None),) * 2,
        check_vma=False,
    )
```

time: 96.9 us -> 63.6 us (0.66)
  Pallas kernels: 0 us -> 59.5 us
  blocking collectives: 31 us -> 0 us
  waiting for transfers between devices: 22 us -> 0 us
  starting transfers between devices: 19.5 us -> 0 us
  matrix products: 12.8 us -> 0 us
  local copies, waits for them, and re-layouts: 8.58 us -> 3.32 us
  other arithmetic: 1.83 us -> 0 us
    pallas_call x0 -> x1, Pallas kernels: none -> 59.5 us  [step(): pl.pallas_call(functools.partial(kernel, n, ns, parts), out_shape=[jax.Sh...]
    all_to_all x1 -> x0, blocking collectives: 31 us -> none  [on_device(): lax.all_to_all(green_blocks, 'energy', split_axis=2, concat_axis=0, tiled...]
    ppermute x5 -> x0, starting transfers between devices: 15.3 us -> none  [the longest x3 8.13 us: from_behind(): return lax.ppermute(block, axis, route)]
    ppermute x5 -> x0, waiting for transfers between devices: 13.2 us -> none  [the longest x1 6.93 us: with_halo(): before = lax.ppermute(last, axis, up)]
    dot_general x6 -> x0, matrix products: 12.8 us -> none  [the longest x1 3.45 us: dress_upper(): jnp.einsum('ij,ejk->eik', link, inner, preferred_element_type=jnp.float32)]
    all_to_all x1 -> x0, waiting for transfers between devices: 8.81 us -> none  [on_device(): lax.all_to_all(polar_rows, 'energy', split_axis=0, concat_axis=2, tiled=T...]
    all_to_all x1 -> x0, starting transfers between devices: 4.14 us -> none  [on_device(): lax.all_to_all(polar_rows, 'energy', split_axis=0, concat_axis=2, tiled=T...]
    unnamed x11 -> x4, local copies, waits for them, and re-layouts: 6.91 us -> 3.32 us
  transfers between devices with their start and end apart: 6 -> 0, of which waited for: 4 -> 0; matrix products, arithmetic and copies ran while one was open for 11% -> 0% of each run, Pallas kernels for 0% -> 0%
where the time goes in v1:
time: 63.6 us; the launch traced here: 63.5 us
  Pallas kernels  59.5 us (94%)
  local copies, waits for them, and re-layouts  3.32 us (5%)
  between operations  0.65 us (1%)
    pallas_call x1, Pallas kernels, step(): pl.pallas_call(functools.partial(kernel, n, ns, parts), out_shape=[jax.Sh...  59.5 us
    unnamed x4, local copies, waits for them, and re-layouts  3.32 us

profile of v1, /device:TPU:1, one launch (start us, length us, event | category | flops | bytes accessed | tf_op | source)
XLA Modules:
  0.0 63.5 jit_solution(1820710915446760838)
XLA Ops:
  0.6 59.5 %shard_map.50 = (bf16[2,1,512,512]{3,2,1,0:T(8,128)(2,1)}, bf16[2,1,512,512]{3,2,1,0:T(8,128)(2,1)}) custom-call(bf16[2,1,512,512]{3,2,1,0:T(8,128)(2,1)} %green.1, bf16[1,512,512]{2,1,0:T(8,128)(2,1)} %coupling.1, bf16[1,512,512]{2,1,0:T(8,128)(2,1)} %coulomb.1), custom_call_target="tpu_custom_call" | custom-call | tf_op jit(solution)/shard_map/pallas_call | solution.py:268
  60.1 0.0 copy-start
  60.1 2.4 %copy.7 = bf16[2,1,512,512]{3,2,1,0:T(8,128)(2,1)} copy(bf16[2,1,512,512]{3,2,1,0:T(8,128)(2,1)} %get-tuple-element.4) | data formatting | bytes 2097152
  62.5 0.0 copy-done
  62.5 1.0 %copy.8 = bf16[2,1,512,512]{3,2,1,0:T(8,128)(2,1)} copy(bf16[2,1,512,512]{3,2,1,0:T(8,128)(2,1)S(1)} %copy-done) | data formatting | bytes 2097152
Async XLA Ops:
  60.1 2.4 %copy-start = (bf16[2,1,512,512]{3,2,1,0:T(8,128)(2,1)S(1)}, bf16[2,1,512,512]{3,2,1,0:T(8,128)(2,1)}, u32[]{:S(2)}) copy-start(bf16[2,1,512,512]{3,2,1,0:T(8,128)(2,1)} %get-tuple-element.5) | copy-start | bytes 3145732

commit v2 on v1

--- a/solution.py
+++ b/solution.py
@@ -60,8 +60,8 @@
 
 
 def kernel(
-    n, ns, parts, green, coupling, coulomb, sigma_out, screen_out,
-    g, h, c, gath, prow, pol, inner, rim_b, rim_a, g_above, low_in, low_out, sigma, screen,
+    n, ns, parts, green, coupling, coulomb, sigma, screen,
+    g, h, c, gath, prow, pol, inner, rim_b, rim_a, g_above, low_in, low_out, outer,
     local, ss1, rs1, ss2, rs2, ssb, rsb, ssa, rsa, sside, rside,
 ):
     per, m = g.shape[0], g.shape[1]
@@ -163,7 +163,7 @@
         def upper(e, _):
             mid = matmul(g_above[e], h[...], 1, 1).astype(BF16)
             term = matmul(h[...], mid).astype(BF16)
-            sigma[e] = (low_in[e].astype(F32) + term.astype(F32)).astype(BF16)
+            sigma[e, 0] = (low_in[e].astype(F32) + term.astype(F32)).astype(BF16)
             return 0
 
         lax.fori_loop(0, per, upper, 0)
@@ -201,8 +201,6 @@
             second[part, i].start()
         forward(part, 0)
     self_energy()
-    sigma_store = pltpu.make_async_copy(sigma, sigma_out.at[:, 0], local.at[0])
-    sigma_store.start()
 
     loads[2].wait()
     for part in range(parts):
@@ -217,6 +215,12 @@
 
         lax.fori_loop(0, per, screen_inner, 0)
 
+    def screen_outer(e, _):
+        outer[e] = matmul(c[...], inner[e])
+        return 0
+
+    lax.fori_loop(0, per, screen_outer, 0)
+
     for copies in rims.values():
         @pl.when(has_down)
         def _():
@@ -226,12 +230,9 @@
         def _():
             copies[1].wait_recv()
 
-    stores = []
     for e in range(per):
         beside = rim_b[e].astype(F32) + rim_a[e].astype(F32)
-        screen[e] = (matmul(c[...], inner[e]) + 0.5 * beside).astype(BF16)
-        stores.append(pltpu.make_async_copy(screen.at[e], screen_out.at[e, 0], local.at[1 + e]))
-        stores[-1].start()
+        screen[e, 0] = (outer[e] + 0.5 * beside).astype(BF16)
 
     for copy in list(first.values()) + list(second.values()):
         copy.wait_send()
@@ -248,8 +249,15 @@
         for copies in rims.values():
             copies[1].wait_send()
 
-    sigma_store.wait()
-    for copy in stores:
+
+def store(sigma, screen, sigma_out, screen_out, sems):
+    copies = [
+        pltpu.make_async_copy(sigma, sigma_out, sems.at[0]),
+        pltpu.make_async_copy(screen, screen_out, sems.at[1]),
+    ]
+    for copy in copies:
+        copy.start()
+    for copy in copies:
         copy.wait()
 
 
@@ -258,27 +266,42 @@
 
     def step(green, coupling, coulomb):
         per, m, count = green.shape[0], green.shape[-1], green.shape[0] * n
-        parts = 2 if m // n % (2 * TILE) == 0 else 1
+        parts = max(k for k in (1, 2) if m // n % (k * TILE) == 0)
         rows = m // n
         blocks = pltpu.VMEM((per, m, m), BF16)
         square = pltpu.VMEM((m, m), BF16)
         strip = pltpu.VMEM((count, rows, m), BF16)
         sems = pltpu.SemaphoreType.DMA((parts, n))
-        anywhere = pl.BlockSpec(memory_space=pl.ANY)
-        return tuple(pl.pallas_call(
+        shapes = [jax.ShapeDtypeStruct(green.shape, BF16)] * 2
+        near = pl.BlockSpec(memory_space=pltpu.VMEM)
+        far = pl.BlockSpec(memory_space=pltpu.HBM)
+        held = pl.pallas_call(
             functools.partial(kernel, n, ns, parts),
-            out_shape=[jax.ShapeDtypeStruct(green.shape, BF16)] * 2,
-            in_specs=[anywhere] * 3,
-            out_specs=[anywhere] * 2,
+            out_shape=shapes,
+            in_specs=[far] * 3,
+            out_specs=[near] * 2,
             scratch_shapes=[blocks, square, square, strip, strip]
-            + [blocks] * 9
-            + [pltpu.SemaphoreType.DMA((max(3 + parts, 1 + per),))]
+            + [blocks] * 6
+            + [blocks, pltpu.VMEM((per, m, m), F32)]
+            + [pltpu.SemaphoreType.DMA((3 + parts,))]
             + [sems] * 8
             + [pltpu.SemaphoreType.DMA((2,))] * 2,
             compiler_params=pltpu.CompilerParams(
-                collective_id=0, has_side_effects=True, vmem_limit_bytes=67043328
+                collective_id=0, has_side_effects=True, vmem_limit_bytes=40 * 1024 * 1024
             ),
-        )(green, coupling, coulomb))
+            name="step",
+        )(*(pltpu.with_memory_space_constraint(x, pltpu.HBM) for x in (green, coupling, coulomb)))
+        return tuple(
+            pl.pallas_call(
+                store,
+                out_shape=shapes,
+                in_specs=[near] * 2,
+                out_specs=[far] * 2,
+                scratch_shapes=[pltpu.SemaphoreType.DMA((2,))],
+                compiler_params=pltpu.CompilerParams(vmem_limit_bytes=8 * 1024 * 1024),
+                name="store",
+            )(*held)
+        )
 
     placed = (P("energy", "slab", None, None), P("slab", None, None), P("slab", None, None))
     return jax.shard_map(

time: 63.6 us -> 60.6 us (0.953)
  local copies, waits for them, and re-layouts: 3.32 us -> 0 us
    unnamed x4 -> x0, local copies, waits for them, and re-layouts: 3.32 us -> none
    pallas_call x1 -> x2, Pallas kernels: 59.5 us -> 59.8 us  [the longest x1 58.4 us: step(): pl.pallas_call(functools.partial(kernel, n, ns, parts), out_shape=shapes,...]
where the time goes in v2:
time: 60.6 us; the launch traced here: 60.4 us
  Pallas kernels  59.8 us (99%)
  between operations  0.64 us (1%)
    pallas_call x1, Pallas kernels, step(): pl.pallas_call(functools.partial(kernel, n, ns, parts), out_shape=shapes,...  58.4 us
    pallas_call x1, Pallas kernels, step(): pl.pallas_call(store, out_shape=shapes, in_specs=[near] * 2, out_specs=[f...  1.33 us

profile of v2, /device:TPU:1, one launch (start us, length us, event | category | flops | bytes accessed | tf_op | source)
XLA Modules:
  0.0 60.4 jit_solution(940971523650222678)
XLA Ops:
  0.6 58.4 %step.1 = (bf16[2,1,512,512]{3,2,1,0:T(8,128)(2,1)S(1)}, bf16[2,1,512,512]{3,2,1,0:T(8,128)(2,1)S(1)}) custom-call(bf16[2,1,512,512]{3,2,1,0:T(8,128)(2,1)} %green.1, bf16[1,512,512]{2,1,0:T(8,128)(2,1)} %coupling.1, bf16[1,512,512]{2,1,0:T(8,128)(2,1)} %coulomb.1), custom_call_target="tpu_custom_call" | custom-call | tf_op jit(solution)/shard_map/step/pallas_call | solution.py:278
  59.1 1.3 %store.1 = (bf16[2,1,512,512]{3,2,1,0:T(8,128)(2,1)}, bf16[2,1,512,512]{3,2,1,0:T(8,128)(2,1)}) custom-call(bf16[2,1,512,512]{3,2,1,0:T(8,128)(2,1)S(1)} %get-tuple-element.4.sigma, bf16[2,1,512,512]{3,2,1,0:T(8,128)(2,1)S(1)} %get-tuple-element.5.screen), custom_call_target="tpu_custom_call" | custom-call | tf_op jit(solution)/shard_map/store/pallas_call | solution.py:295

commit v3 on v2

--- a/solution.py
+++ b/solution.py
@@ -69,7 +69,16 @@
     me, slab = lax.axis_index("energy"), lax.axis_index("slab")
     up, down = jnp.minimum(slab + 1, ns - 1), jnp.maximum(slab - 1, 0)
     has_up, has_down = slab < ns - 1, slab > 0
-    order = sorted(range(1, n), key=lambda i: abs(2 * i - n))
+    order = range(1, n)
+
+    def partner(i):
+        other, bit = me, 1
+        while bit <= i:
+            if i & bit:
+                other = other + bit * (1 - 2 * (me // bit % 2))
+            bit *= 2
+        return other
+
 
     def block(part, owner):
         return pl.ds(pl.multiple_of(part * (m // parts) + owner * rows, rows), rows)
@@ -113,7 +122,7 @@
     first = {}
     for part in range(parts):
         for i in order:
-            to = (me + i) % n
+            to = partner(i)
             first[part, i] = remote(
                 g.at[:, block(part, to)],
                 gath.at[pl.ds(me * per, per), pl.ds(part * rows, rows)],
@@ -171,7 +180,7 @@
     second, rims = {}, {}
 
     def forward(part, i):
-        piece = block(part, (me - i + n) % n)
+        piece = block(part, partner(i))
         rims[part, i] = (
             remote(pol.at[:, piece], rim_b.at[:, piece], ssb.at[part, i], rsb.at[part, i], {"slab": up}),
             remote(pol.at[:, piece], rim_a.at[:, piece], ssa.at[part, i], rsa.at[part, i], {"slab": down}),
@@ -193,14 +202,15 @@
         span = pl.ds(part * rows, rows)
         pol[:, block(part, me)] = prow[pl.ds(me * per, per), span]
         for i in order:
-            to = (me + i) % n
+            to = partner(i)
             second[part, i] = remote(
                 prow.at[pl.ds(to * per, per), span], pol.at[:, block(part, me)],
                 ss2.at[part, i], rs2.at[part, i], {"energy": to},
             )
             second[part, i].start()
         forward(part, 0)
-    self_energy()
+        if part == 0:
+            self_energy()
 
     loads[2].wait()
     for part in range(parts):
@@ -221,18 +231,20 @@
 
     lax.fori_loop(0, per, screen_outer, 0)
 
-    for copies in rims.values():
-        @pl.when(has_down)
-        def _():
-            copies[0].wait_recv()
-
-        @pl.when(has_up)
-        def _():
-            copies[1].wait_recv()
-
-    for e in range(per):
-        beside = rim_b[e].astype(F32) + rim_a[e].astype(F32)
-        screen[e, 0] = (outer[e] + 0.5 * beside).astype(BF16)
+    for part in range(parts):
+        for i in range(n):
+            @pl.when(has_down)
+            def _():
+                rims[part, i][0].wait_recv()
+
+            @pl.when(has_up)
+            def _():
+                rims[part, i][1].wait_recv()
+
+        half = pl.ds(part * (m // parts), m // parts)
+        for e in range(per):
+            beside = rim_b[e, half].astype(F32) + rim_a[e, half].astype(F32)
+            screen[e, 0, half] = (outer[e, half] + 0.5 * beside).astype(BF16)
 
     for copy in list(first.values()) + list(second.values()):
         copy.wait_send()
@@ -263,6 +275,7 @@
 
 def solution(mesh):
     n, ns = mesh.shape["energy"], mesh.shape["slab"]
+    assert n & (n - 1) == 0
 
     def step(green, coupling, coulomb):
         per, m, count = green.shape[0], green.shape[-1], green.shape[0] * n

time: 60.6 us -> 58.6 us (0.967)
  Pallas kernels: 59.8 us -> 57.8 us
    pallas_call x1, Pallas kernels: 58.4 us -> 56.5 us  [step(): pl.pallas_call(functools.partial(kernel, n, ns, parts), out_shape=shapes,...]
where the time goes in v3:
time: 58.6 us; the launch traced here: 58.5 us
  Pallas kernels  57.8 us (99%)
  between operations  0.64 us (1%)
    pallas_call x1, Pallas kernels, step(): pl.pallas_call(functools.partial(kernel, n, ns, parts), out_shape=shapes,...  56.5 us
    pallas_call x1, Pallas kernels, step(): pl.pallas_call(store, out_shape=shapes, in_specs=[near] * 2, out_specs=[f...  1.33 us

profile of v3, /device:TPU:1, one launch (start us, length us, event | category | flops | bytes accessed | tf_op | source)
XLA Modules:
  0.0 58.5 jit_solution(842265810306560317)
XLA Ops:
  0.6 56.5 %step.1 = (bf16[2,1,512,512]{3,2,1,0:T(8,128)(2,1)S(1)}, bf16[2,1,512,512]{3,2,1,0:T(8,128)(2,1)S(1)}) custom-call(bf16[2,1,512,512]{3,2,1,0:T(8,128)(2,1)} %green.1, bf16[1,512,512]{2,1,0:T(8,128)(2,1)} %coupling.1, bf16[1,512,512]{2,1,0:T(8,128)(2,1)} %coulomb.1), custom_call_target="tpu_custom_call" | custom-call | tf_op jit(solution)/shard_map/step/pallas_call | solution.py:291
  57.1 1.3 %store.1 = (bf16[2,1,512,512]{3,2,1,0:T(8,128)(2,1)}, bf16[2,1,512,512]{3,2,1,0:T(8,128)(2,1)}) custom-call(bf16[2,1,512,512]{3,2,1,0:T(8,128)(2,1)S(1)} %get-tuple-element.4.sigma, bf16[2,1,512,512]{3,2,1,0:T(8,128)(2,1)S(1)} %get-tuple-element.5.screen), custom_call_target="tpu_custom_call" | custom-call | tf_op jit(solution)/shard_map/store/pallas_call | solution.py:308
